TPU v7x, 32 devices: a whole 2x2x4 slice. The times are simulated.
32 devices in a mesh: seq: 8 (over y, x, core), exp: 4 (over z).
Axes of the slice: x: 2, y: 2, z: 4, core: 2. Of those that a mesh axis runs over, the one named last changes fastest.
Arguments:
- grad_out: bfloat16 [4096, 2048], P(('seq', 'exp')), may hold values from -6 to 6
- out_proj: bfloat16 [4096, 2048], P('exp'), may hold values from -0.125 to 0.125
- step_size: float32 [64, 4096], P('exp', 'seq'), may hold values from 0.001 to 0.1
- log_decay: float32 [64, 4096], P('exp', 'seq'), may hold values from -1 to 0, as said below
- b_input: float32 [16, 4096], P(None, 'seq'), may hold values from -1.5 to 1.5
- c_output: float32 [16, 4096], P(None, 'seq'), may hold values from -1.5 to 1.5
- skip_gain: float32 [4096], P('exp'), may hold values from 0.5 to 1.5
- expert_ids: int32 [4096, 2], P('seq'), may hold values from 0 to 3, all different within a row; in each aligned block of 128 rows (0 to 127, 128 to 255, ...) at most 66 rows name the same one
- hidden_act: bfloat16 [4, 32, 66, 8192], P('exp', None, None, 'seq'), may hold values from -6 to 6
- w_down: bfloat16 [4, 8192, 2048], P('exp', 'seq'), may hold values from -0.0029296875 to 0.0029296875
Outputs:
- d_inner: bfloat16 [4096, 4096], P('seq', 'exp')
- d_gate: float32 [2, 4096], P(None, ('seq', 'exp'))
Inputs may be any that keep to these rules, and one draw needn't show every extreme that they name: `expert_ids`: each row names 2 different experts. Within the rows of one token group no expert is named by more than 66 rows, and in every draw some expert is named by exactly 66 rows of some group. `log_decay`: every entry is negative.
All inputs are finite; a program needn't handle non-finite values.
Results may differ from a plain program's by a relative error of at most 0.00065.
Values may be sent and summed in bfloat16 or wider, within the bound.
A program may use at most 128 MiB of HBM per device.

v0:
```python
import jax
import jax.numpy as jnp
from jax import lax
from jax.sharding import PartitionSpec as P

HEAD = 64


highest = lax.Precision.HIGHEST


def block_pass(state_in, pieces):
    grad_block, decay_block, step_block, b_block, c_block = pieces
    cum_decay = jnp.cumsum(decay_block, axis=1)
    gap_table = cum_decay[:, None, :] - cum_decay[:, :, None]
    upper_mask = lax.broadcasted_iota(jnp.int32, gap_table.shape, 2) >= lax.broadcasted_iota(
        jnp.int32, gap_table.shape, 1
    )
    weights = jnp.where(upper_mask, jnp.exp(jnp.where(upper_mask, gap_table, 0.0)), 0.0)
    intersection = lax.dot_general(
        b_block,
        c_block,
        (((0,), (0,)), ((), ())),
        precision=highest,
        preferred_element_type=jnp.float32,
    )
    within = jnp.einsum("hut,thp->uhp", weights * intersection[None], grad_block, precision=highest)
    tail_decay = jnp.exp(cum_decay[:, -1:] - cum_decay)
    from_state = (
        jnp.einsum("nu,hnp->uhp", b_block, state_in, precision=highest) * tail_decay.T[:, :, None]
    )
    result = step_block.T[:, :, None] * (within + from_state)
    state_out = jnp.einsum(
        "ht,nt,thp->hnp", jnp.exp(cum_decay), c_block, grad_block, precision=highest
    )
    state_out = state_out + jnp.exp(cum_decay[:, -1])[:, None, None] * state_in
    return (state_out, result)


def local_sweep(grad_rows, decay_rows, step_rows, b_rows, c_rows, start_state):
    row_count = grad_rows.shape[0]
    head_count = decay_rows.shape[0]
    block_len = min(512, row_count)
    block_count = row_count // block_len
    pieces = (
        grad_rows.reshape(block_count, block_len, head_count, grad_rows.shape[2]),
        decay_rows.reshape(head_count, block_count, block_len).transpose(1, 0, 2),
        step_rows.reshape(head_count, block_count, block_len).transpose(1, 0, 2),
        b_rows.reshape(b_rows.shape[0], block_count, block_len).transpose(1, 0, 2),
        c_rows.reshape(c_rows.shape[0], block_count, block_len).transpose(1, 0, 2),
    )
    state_out, results = lax.scan(block_pass, start_state, pieces, reverse=True)
    return (state_out, results.reshape(row_count, head_count, grad_rows.shape[2]))


def route_table(groups, expert, cap_len):
    hit_mask = jnp.any(groups == expert, axis=2)
    rank_ids = jnp.cumsum(hit_mask.astype(jnp.int32), axis=1) - 1
    slot_ids = lax.broadcasted_iota(jnp.int32, (1, 1, cap_len), 2)
    chosen = jnp.logical_and(hit_mask[:, :, None], rank_ids[:, :, None] == slot_ids)
    token_ids = lax.broadcasted_iota(jnp.int32, chosen.shape, 1)
    position = jnp.sum(jnp.where(chosen, token_ids, 0), axis=1)
    filled = jnp.any(chosen, axis=1)
    return (position, filled)


def slot_lookup(slot_table, own_ids, cap_len, expert_count):
    experts_iota = lax.broadcasted_iota(jnp.int32, (1, 1, expert_count), 2)
    onehot = own_ids[:, :, None] == experts_iota
    member = jnp.any(onehot, axis=1).astype(jnp.int32)
    rank_ids = jnp.cumsum(member, axis=0) - 1
    slot_of = jnp.sum(jnp.where(onehot, rank_ids[:, None, :], 0), axis=2)
    picked = jnp.sum(jnp.where(onehot[:, :, :, None], slot_table[None, None], 0.0), axis=2)
    slot_iota = lax.broadcasted_iota(jnp.int32, (1, 1, cap_len), 2)
    return jnp.sum(jnp.where(slot_of[:, :, None] == slot_iota, picked, 0.0), axis=2)


def shards(
    grad_out,
    out_proj,
    step_size,
    log_decay,
    b_input,
    c_output,
    skip_gain,
    expert_ids,
    hidden_act,
    w_down,
):
    exp_index = lax.axis_index("exp")
    seq_index = lax.axis_index("seq")
    exp_count = lax.axis_size("exp")
    seq_count = lax.axis_size("seq")
    tok_len = grad_out.shape[0]
    cap_len = hidden_act.shape[2]
    gathered = lax.all_gather(grad_out, "exp", axis=0, tiled=True)
    groups = expert_ids.reshape(exp_count, tok_len, expert_ids.shape[1])
    position, filled = route_table(groups, exp_index, cap_len)
    flat_index = (position + lax.broadcasted_iota(jnp.int32, position.shape, 0) * tok_len).reshape(
        -1
    )
    slot_rows = jnp.take(gathered, flat_index, axis=0)
    slot_rows = jnp.where(filled.reshape(-1, 1), slot_rows, jnp.zeros_like(slot_rows))
    saved_rows = hidden_act.reshape(-1, hidden_act.shape[3])
    weights = w_down[0]
    projected = lax.dot_general(
        lax.all_gather(slot_rows, "seq", axis=0, tiled=True),
        weights,
        (((1,), (1,)), ((), ())),
        preferred_element_type=jnp.float32,
    )
    partial_scores = jnp.sum(projected * saved_rows.astype(jnp.float32), axis=1)
    head_count = out_proj.shape[0] // HEAD
    inner_grad = lax.dot_general(
        gathered, out_proj, (((1,), (1,)), ((), ())), preferred_element_type=jnp.float32
    )
    row_count = inner_grad.shape[0]
    start_state = jnp.zeros((head_count, b_input.shape[0], HEAD), jnp.float32)
    summary, swept_part = local_sweep(
        inner_grad.reshape(row_count, head_count, HEAD),
        log_decay,
        step_size,
        b_input,
        c_output,
        start_state,
    )
    total_decay = jnp.sum(log_decay, axis=1)
    all_states, all_decay = (
        lax.all_gather(summary[None], "seq", axis=0, tiled=True),
        lax.all_gather(total_decay[None], "seq", axis=0, tiled=True),
    )
    shard_ids = lax.broadcasted_iota(jnp.int32, all_decay.shape, 0)
    beyond = jnp.where(shard_ids > seq_index, all_decay, 0.0)
    exponent = jnp.cumsum(beyond, axis=0) - beyond
    factor = jnp.where(
        shard_ids > seq_index, jnp.exp(jnp.where(shard_ids > seq_index, exponent, 0.0)), 0.0
    )
    incoming = jnp.sum(factor[:, :, None, None] * all_states, axis=0)
    suffix = jnp.flip(jnp.cumsum(jnp.flip(log_decay, 1), axis=1), 1) - log_decay
    from_carry = (
        jnp.einsum("nu,hnp->uhp", b_input, incoming, precision=highest)
        * jnp.exp(suffix).T[:, :, None]
    )
    combined = swept_part + step_size.T[:, :, None] * from_carry
    d_inner = (combined.reshape(row_count, -1) + skip_gain * inner_grad).astype(jnp.bfloat16)
    summed = lax.psum_scatter(
        partial_scores.reshape(seq_count, exp_count, cap_len),
        "seq",
        scatter_dimension=0,
        tiled=True,
    )
    slot_table = lax.all_to_all(
        summed.reshape(exp_count, 1, cap_len), "exp", split_axis=0, concat_axis=1, tiled=True
    ).reshape(exp_count, cap_len)
    own_ids = lax.dynamic_slice_in_dim(expert_ids, exp_index * tok_len, tok_len, 0)
    d_gate = slot_lookup(slot_table, own_ids, cap_len, exp_count).T
    return (d_inner, d_gate)


def solution(mesh):
    in_specs = (
        P(("seq", "exp"), None),
        P("exp", None),
        P("exp", "seq"),
        P("exp", "seq"),
        P(None, "seq"),
        P(None, "seq"),
        P("exp"),
        P("seq", None),
        P("exp", None, None, "seq"),
        P("exp", "seq", None),
    )
    out_specs = (P("seq", "exp"), P(None, ("seq", "exp")))
    return jax.shard_map(shards, mesh=mesh, in_specs=in_specs, out_specs=out_specs, check_vma=False)
```

profile of v0, /device:TPU:0, one launch (start us, length us, event | category | flops | bytes accessed | tf_op | source)
XLA Modules:
  0.0 207.7 jit_solution(10610763480653563069)
XLA Ops:
  7.2 0.7 all-gather.5.cloned.1.call-update
  8.0 0.7 compare_reduce_fusion
  8.7 0.3 reduce_window_sum.73
  9.0 1.2 select_reduce_fusion.1
  10.5 1.2 fusion.21
  12.0 46.0 %all-gather.5.cloned.1.call-done = bf16[512,2048]{1,0:T(8,128)(2,1)} async-done(((bf16[128,2048]{1,0:T(8,128)(2,1)}), bf16[512,2048]{1,0:T(8,128)(2,1)}) %all-gather.5.cloned.1.call-update) | async-done | bytes 2097168 | tf_op jit(solution)/shard_map/all_gather | solution.py:96
  58.0 6.2 %gather_fusion = bf16[264,2048]{1,0:T(8,128)(2,1)S(1)} fusion(bf16[512,2048]{1,0:T(8,128)(2,1)} %all-gather.5.cloned.1.call-done, s32[1024]{0:T(1024)S(1)} %pad_clamp_fusion), kind=kCustom, calls=%fused_computation | custom fusion | bytes 2163744 | tf_op jit(solution)/shard_map/jit(_take)/gather | solution.py:102
  64.2 1.2 select_select_fusion
  65.5 0.3 rev.7
  65.8 1.1 reduce-window.14
  67.1 1.2 reduce-window.16
  68.9 8.6 %copy.85 = f32[1,32,66,1024]{3,2,1,0:T(8,128)} copy(bf16[1,32,66,1024]{3,1,2,0:T(8,128)(2,1)} %param.18) | data formatting | bytes 12976128 | tf_op jit(solution)/shard_map/convert_element_type | solution.py:112
  77.5 9.5 %reshape.166 = f32[2112,1024]{1,0:T(8,128)} reshape(f32[1,32,66,1024]{3,2,1,0:T(8,128)} %copy.85) | data formatting | bytes 17301504 | tf_op jit(solution)/shard_map/convert_element_type | solution.py:112
  87.0 0.8 constant_dynamic-slice_fusion.1
  88.2 0.6 fusion.31
  90.2 2.0 fusion.33
  92.2 3.1 %fusion.22 = f32[16,64,512]{2,1,0:T(8,128)} fusion(f32[16,512]{1,0:T(8,128)S(1)} %copy-done), kind=kOutput, calls=%fused_computation.34 | convolution fusion | flops 100663296 | bytes 2129920 | tf_op jit(solution)/shard_map/while/body/eval_jaxpr/nu,hnp->uhp/dot_general | solution.py:30
  95.3 5.9 %fusion.32 = f32[512,1024]{1,0:T(8,128)} fusion(bf16[512,2048]{1,0:T(8,128)(2,1)S(1)} %copy-done.1, bf16[1024,2048]{1,0:T(8,128)(2,1)} %param.11), kind=kOutput, calls=%fused_computation.74 | convolution fusion | flops 2147483648 | bytes 8388608 | tf_op jit(solution)/shard_map/dot_general | solution.py:114
  101.2 2.1 %copy.75 = f32[512,1024]{0,1:T(8,128)S(1)} copy(f32[512,1024]{1,0:T(8,128)} %fusion.32) | data formatting | bytes 4194304 | tf_op jit(solution)/shard_map/dot_general | solution.py:114
  103.3 1.8 convolution_add_fusion
  105.1 16.7 %all-gather.1 = f32[128,16,64]{2,1,0:T(8,128)S(1)} all-gather(f32[16,16,64]{2,1,0:T(8,128)S(1)} %convolution_add_fusion), channel_id=3, replica_groups=mesh['seq'=8,'exp'=4] {'seq'}, dimensions={0}, use_global_device_ids=true | all-gather | bytes 589824 | tf_op jit(solution)/shard_map/all_gather | solution.py:129
  121.7 2.2 %all-gather.7.cloned.1.call-done = bf16[2112,2048]{1,0:T(8,128)(2,1)} async-done(((bf16[264,2048]{1,0:T(8,128)(2,1)}), bf16[2112,2048]{1,0:T(8,128)(2,1)}) %all-gather.7.cloned.1.call-update) | async-done | bytes 8650768 | tf_op jit(solution)/shard_map/all_gather | solution.py:107
  123.9 14.9 %multiply_reduce_fusion = f32[2112]{0:T(1024)S(1)} fusion(f32[2112,1024]{1,0:T(8,128)} %reshape.166, bf16[2112,2048]{1,0:T(8,128)(2,1)} %all-gather.7.cloned.1.call-done, bf16[1,1024,2048]{2,1,0:T(8,128)(2,1)} %param.19), kind=kOutput, calls=%fused_computation.8 | convolution fusion | flops 8862693376 | bytes 21504256 | tf_op jit(solution)/shard_map/dot_general | solution.py:106
  139.0 23.5 %all-reduce.2 = (f32[128]{0:T(128)S(1)}, f32[8,4,66]{2,1,0:T(4,128)S(1)}) all-reduce(f32[128]{0:T(128)S(1)} %dynamic-update-slice, f32[8,4,66]{2,1,0:T(4,128)S(1)} %reshape.164), channel_id=2, replica_groups=mesh['seq'=8,'exp'=4] {'seq'}, use_global_device_ids=true, to_apply=%add | all-reduce | flops 2240 | bytes 17920
  163.0 1.8 fusion.24
  164.8 20.5 %fusion.12 = f32[512,16,64]{0,2,1:T(8,128)} fusion(f32[16,64,512]{2,1,0:T(8,128)S(1)} %fusion.24, f32[16,64,512]{2,1,0:T(8,128)S(1)} %copy-done.3, f32[512,16,64]{0,2,1:T(8,128)S(1)} %bitcast.79, f32[512,512]{1,0:T(8,128)S(1)} %copy-done.4, f32[16,512]{1,0:T(8,128)S(1)} %copy_bitcast_fusion.1, f32[512,16]{0,1:T(8,128)S(1)} %get-tuple-element.22, ...), kind=kOutput, calls=%fused_computation.16 | convolution fusion | flops 3244818432 | bytes 9568256 | tf_op jit(solution)/shard_map/while/body/eval_jaxpr/hut,thp->uhp/dot_general | solution.py:27
  185.4 3.0 %copy.80 = f32[512,1024]{1,0:T(8,128)} copy(f32[512,1024]{0,1:T(8,128)} %bitcast.81) | data formatting | bytes 4194304 | tf_op jit(solution)/shard_map/reshape | solution.py:145
  188.4 1.2 constant_dynamic-slice_fusion
  189.6 4.7 %all-to-all-start = ((f32[4,1,66]{2,1,0:T(1,128)}), f32[4,1,66]{2,1,0:T(1,128)S(1)}, u32[]{:S(2)}, u32[]{:S(2)}) async-start(f32[4,1,66]{2,1,0:T(1,128)} %bitcast.17), calls=%async_computation | async-start | bytes 4096 | tf_op jit(solution)/shard_map/all_to_all | solution.py:152
  194.3 3.1 %add_convert_fusion = bf16[512,1024]{1,0:T(8,128)(2,1)} fusion(f32[512,1024]{1,0:T(8,128)} %copy.80, f32[512,1024]{1,0:T(8,128)S(1)} %copy-done.2, f32[1024]{0:T(1024)S(1)} %copy-done.7), kind=kLoop, calls=%fused_computation.19 | loop fusion | flops 1572864 | bytes 5246976 | tf_op jit(solution)/shard_map/convert_element_type | solution.py:145
  197.4 2.5 %all-to-all-done = f32[4,1,66]{2,1,0:T(1,128)S(1)} async-done(((f32[4,1,66]{2,1,0:T(1,128)}), f32[4,1,66]{2,1,0:T(1,128)S(1)}, u32[]{:S(2)}, u32[]{:S(2)}) %all-to-all-start) | async-done | bytes 1088 | tf_op jit(solution)/shard_map/all_to_all | solution.py:152
  200.2 0.6 select_reduce_fusion.2
  (68 shorter events, 3.5 us)
Async XLA Ops:
  7.2 83.1 %copy-start = (f32[16,512]{1,0:T(8,128)S(1)}, f32[16,512]{1,0:T(8,128)}, u32[]{:S(2)}) copy-start(f32[16,512]{1,0:T(8,128)} %param.14) | copy-start | bytes 98308
  7.2 50.8 %all-gather.5.cloned.1.call-start = ((), (), s32[]{:S(2)}) async-start(), calls=%async_computation.1 | async-start | bytes 2621440 | tf_op jit(solution)/shard_map/all_gather | solution.py:96
  7.9 116.0 %all-gather.7.cloned.1.call-start = ((), (), s32[]{:S(2)}) async-start(), calls=%async_computation.2 | async-start | bytes 9732096 | tf_op jit(solution)/shard_map/all_gather | solution.py:107
  64.2 1.3 copy-start.5
  77.5 10.7 %copy-start.8 = (u32[32]{0:T(128)S(1)}, u32[32]{0:T(128)}, u32[]{:S(2)}) copy-start(u32[32]{0:T(128)} %constant.76) | copy-start | bytes 388
  77.5 12.8 %copy-start.6 = (f32[16,512]{1,0:T(8,128)S(1)}, f32[16,512]{1,0:T(8,128)}, u32[]{:S(2)}) copy-start(f32[16,512]{1,0:T(8,128)} %param.15) | copy-start | bytes 98308
  87.0 8.3 %copy-start.1 = (bf16[512,2048]{1,0:T(8,128)(2,1)S(1)}, bf16[512,2048]{1,0:T(8,128)(2,1)}, u32[]{:S(2)}) copy-start(bf16[512,2048]{1,0:T(8,128)(2,1)} %all-gather.5.cloned.1.call-done) | copy-start | bytes 6291460
  138.9 25.9 %copy-start.9 = (f32[16,512]{1,0:T(8,128)S(1)}, f32[16,512]{1,0:T(8,128)}, u32[]{:S(2)}) copy-start(f32[16,512]{1,0:T(8,128)} %param.12) | copy-start | bytes 98308
  162.7 2.2 %copy-start.3 = (f32[16,64,512]{2,1,0:T(8,128)S(1)}, f32[16,64,512]{2,1,0:T(8,128)}, u32[]{:S(2)}) copy-start(f32[16,64,512]{2,1,0:T(8,128)} %fusion.22) | copy-start | bytes 6291460
  162.7 2.2 %copy-start.4 = (f32[512,512]{1,0:T(8,128)S(1)}, f32[512,512]{1,0:T(8,128)}, u32[]{:S(2)}) copy-start(f32[512,512]{1,0:T(8,128)} %fusion.33) | copy-start | bytes 3145732
  185.4 9.0 %copy-start.2 = (f32[512,1024]{1,0:T(8,128)S(1)}, f32[512,1024]{1,0:T(8,128)}, u32[]{:S(2)}) copy-start(f32[512,1024]{1,0:T(8,128)} %fusion.32) | copy-start | bytes 6291460
  185.4 9.0 %copy-start.7 = (f32[1024]{0:T(1024)S(1)}, f32[1024]{0:T(1024)}, u32[]{:S(2)}) copy-start(f32[1024]{0:T(1024)} %param.16) | copy-start | bytes 12292
  189.6 10.3 %all-to-all-start = ((f32[4,1,66]{2,1,0:T(1,128)}), f32[4,1,66]{2,1,0:T(1,128)S(1)}, u32[]{:S(2)}, u32[]{:S(2)}) async-start(f32[4,1,66]{2,1,0:T(1,128)} %bitcast.17), calls=%async_computation | async-start | bytes 4096 | tf_op jit(solution)/shard_map/all_to_all | solution.py:152
Sparse Core Ops, SparseCore 0:
  9.6 48.3 all-gather.4
  65.6 58.3 all-gather.6
where the time goes:
time: 208 us
  waiting for transfers between devices  51.4 us (25%)
  matrix products  50 us (24%)
  blocking collectives  40.1 us (19%)
  local copies, waits for them, and re-layouts  34.5 us (17%)
  between operations  14.9 us (7%)
  other arithmetic  12 us (6%)
  starting transfers between devices  4.76 us (2%)
    all_gather x1, waiting for transfers between devices, shards(): gathered = lax.all_gather(grad_out, 'exp', axis=0, tiled=True)  46 us
    unnamed x1, blocking collectives  23.5 us
    dot_general x1, matrix products, block_pass(): jnp.einsum('hut,thp->uhp', weights * intersection[None], grad_block, prec...  20.5 us
    convert_element_type x2, local copies, waits for them, and re-layouts, shards(): partial_scores = jnp.sum(projected * saved_rows.astype(jnp.float32), axis=1)  18.1 us
    all_gather x1, blocking collectives, shards(): lax.all_gather(summary[None], 'seq', axis=0, tiled=True)  16.7 us
    dot_general x1, matrix products, shards(): lax.dot_general(lax.all_gather(slot_rows, 'seq', axis=0, tiled=True), wei...  14.9 us
    gather x1, local copies, waits for them, and re-layouts, shards(): slot_rows = jnp.take(gathered, flat_index, axis=0)  6.22 us
    dot_general x1, matrix products, shards(): lax.dot_general(gathered, out_proj, (((1,), (1,)), ((), ())), preferred_e...  5.91 us
  transfers between devices with their start and end apart: 3, of which 3 were waited for; matrix products, arithmetic and copies ran while one was open for 22% of the time, Pallas kernels for 0%

commit v1 on v0

--- a/solution.py
+++ b/solution.py
@@ -1,6 +1,10 @@
+import functools
+
 import jax
 import jax.numpy as jnp
 from jax import lax
+from jax.experimental import pallas as pl
+from jax.experimental.pallas import tpu as pltpu
 from jax.sharding import PartitionSpec as P
 
 HEAD = 64
@@ -157,6 +161,470 @@
     return (d_inner, d_gate)
 
 
+VMEM_ROOM = 60 << 20
+BF = jnp.bfloat16
+F32 = jnp.float32
+
+
+def halves(x):
+    top = x.astype(BF)
+    return top, (x - top.astype(F32)).astype(BF)
+
+
+def dot(x, y, dims=((1,), (0,)), precision=None):
+    return lax.dot_general(x, y, (dims, ((), ())), precision=precision, preferred_element_type=F32)
+
+
+def flip(index, bit):
+    return index + bit - 2 * bit * ((index // bit) % 2)
+
+
+def column(table, h):
+    lanes = lax.broadcasted_iota(jnp.int32, table.shape, 1)
+    return jnp.sum(jnp.where(lanes == h, table, 0.0), axis=1, keepdims=True)
+
+
+def fused(
+    sizes,
+    grad_hbm, proj_hbm, hid_hbm, down_hbm, step_ref, decay_ref, b_ref, c_ref, skip_ref, ids_ref,
+    out_ref, score_ref,
+    gath, proj, hid, down, y_ref, rows, hid_pad, pick, inner, fac, acc,
+    cum_ref, cum_t, step_t, b_t, bc, agg, got, carry,
+    load_sem, hid_sem, down_sem, proj_sem,
+    zs_sem, zr_sem, xs_sem, xr_sem, as_sem, ar_sem,
+):
+    n_seq, n_exp, tok, cap, pad, chunks, width = sizes
+    me = lax.axis_index("seq")
+    z = lax.axis_index("exp")
+    shard = n_exp * pad
+    row_count = n_exp * tok
+    bits = [1 << i for i in range(1, n_seq.bit_length() - 1)]
+    n_stage = len(bits)
+    steps = n_exp - 1
+    block = bc.shape[1]
+    blocks = row_count // block
+    channels = inner.shape[1]
+    lane = 2 * HEAD
+    pairs = channels // lane
+
+    for k in range(chunks):
+        pltpu.make_async_copy(
+            grad_hbm.at[:, pl.ds(k * width, width)], gath.at[k, z], load_sem.at[k]
+        ).start()
+    down_copy = pltpu.make_async_copy(down_hbm.at[0], down, down_sem)
+    down_copy.start()
+    hid_copy = pltpu.make_async_copy(hid_hbm.at[0], hid, hid_sem)
+    hid_copy.start()
+    for k in range(chunks):
+        pltpu.make_async_copy(
+            proj_hbm.at[:, pl.ds(k * width, width)], proj.at[k], proj_sem.at[k]
+        ).start()
+
+    barrier = pltpu.get_barrier_semaphore()
+    for bit in [1] + bits:
+        pl.semaphore_signal(barrier, inc=1, device_id={"seq": flip(me, bit)})
+
+    @pl.when(z > 0)
+    def _():
+        pl.semaphore_signal(barrier, inc=1, device_id={"exp": z - 1})
+
+    @pl.when(z < n_exp - 1)
+    def _():
+        pl.semaphore_signal(barrier, inc=1, device_id={"exp": z + 1})
+
+    ends = jnp.minimum(z, 1) + jnp.minimum(n_exp - 1 - z, 1)
+    pl.semaphore_wait(barrier, n_stage + 1 + ends)
+
+    def z_copy(side, k, d, owner, target):
+        return pltpu.make_async_remote_copy(
+            src_ref=gath.at[k, owner],
+            dst_ref=gath.at[k, owner],
+            send_sem=zs_sem.at[side, k, d],
+            recv_sem=zr_sem.at[side, k, d],
+            device_id={"exp": target},
+        )
+
+    def z_send(k, d):
+        @pl.when(jnp.logical_and(z < n_exp - 1, z - d >= 0))
+        def _():
+            z_copy(0, k, d, z - d, z + 1).start()
+
+        @pl.when(jnp.logical_and(z > 0, z + d < n_exp))
+        def _():
+            z_copy(1, k, d, z + d, z - 1).start()
+
+    def z_sent(k, d):
+        @pl.when(jnp.logical_and(z < n_exp - 1, z - d >= 0))
+        def _():
+            z_copy(0, k, d, z - d, z + 1).wait_send()
+
+        @pl.when(jnp.logical_and(z > 0, z + d < n_exp))
+        def _():
+            z_copy(1, k, d, z + d, z - 1).wait_send()
+
+    def z_take(k, d):
+        @pl.when(z - d >= 0)
+        def _():
+            z_copy(0, k, d - 1, z - d, z).wait_recv()
+
+        @pl.when(z + d < n_exp)
+        def _():
+            z_copy(1, k, d - 1, z + d, z).wait_recv()
+
+    for k in range(chunks):
+        pltpu.make_async_copy(
+            grad_hbm.at[:, pl.ds(k * width, width)], gath.at[k, z], load_sem.at[k]
+        ).wait()
+        z_send(k, 0)
+
+    def bit_of(k, stage):
+        if stage == n_stage:
+            return 1
+        low, high = bits[stage], bits[n_stage - 1 - stage]
+        return low + (high - low) * (k % 2)
+
+    def x_copies(k, stage, here):
+        masks = [()]
+        for i in range(stage):
+            masks = masks + [m + (i,) for m in masks]
+        copies = []
+        for j, mask in enumerate(masks):
+            owner = me
+            for i in mask:
+                owner = flip(owner, bit_of(k, i))
+            slot = (1 << stage) - 1 + j
+            if not here:
+                owner = flip(owner, bit_of(k, stage))
+            copies.append(pltpu.make_async_remote_copy(
+                src_ref=rows.at[k, owner],
+                dst_ref=rows.at[k, owner],
+                send_sem=xs_sem.at[k, slot],
+                recv_sem=xr_sem.at[k, slot],
+                device_id={"seq": flip(me, bit_of(k, stage))},
+            ))
+        return copies
+
+    def x_start(k, stage):
+        for mine in x_copies(k, stage, True):
+            mine.start()
+
+    def x_take(k, stage):
+        for theirs in x_copies(k, stage, False):
+            theirs.wait_recv()
+
+    ids = ids_ref[...]
+    hit = jnp.where(jnp.logical_or(ids[:, 0:1] == z, ids[:, 1:2] == z), 1.0, 0.0)
+    for i in range(2, ids.shape[1]):
+        hit = jnp.maximum(hit, jnp.where(ids[:, i : i + 1] == z, 1.0, 0.0))
+    row_id = lax.broadcasted_iota(jnp.int32, (row_count, row_count), 0)
+    col_id = lax.broadcasted_iota(jnp.int32, (row_count, row_count), 1)
+    same = jnp.logical_and(row_id // tok == col_id // tok, col_id < row_id)
+    before = dot(jnp.where(same, 1.0, 0.0).astype(BF), jnp.broadcast_to(hit, (row_count, 128)).astype(BF))
+    group = lax.broadcasted_iota(jnp.int32, (row_count, 1), 0) // tok
+    place = before[:, 0:1].astype(jnp.int32) + group * pad
+    slots = -(-shard // 128) * 128
+    chosen = jnp.logical_and(
+        lax.broadcasted_iota(jnp.int32, (row_count, slots), 1) == place, hit > 0.5
+    )
+    pick[...] = jnp.transpose(jnp.where(chosen, 1.0, 0.0))[:shard].astype(BF)
+
+    tri = jnp.where(row_id <= col_id, 1.0, 0.0)
+    cum = dot(decay_ref[...], tri, precision=highest)
+    cum_ref[...] = cum
+    cum_t[...] = jnp.transpose(cum)
+    step_t[...] = jnp.transpose(step_ref[...])
+    b_t[...] = jnp.transpose(b_ref[...])
+    keep = lax.broadcasted_iota(jnp.int32, (block, block), 1) >= lax.broadcasted_iota(
+        jnp.int32, (block, block), 0
+    )
+    for i in range(blocks):
+        span = slice(i * block, (i + 1) * block)
+        cross = dot(b_t[span, :], c_ref[:, span], precision=highest)
+        bc[i] = jnp.where(keep, cross, 0.0)
+
+    hid_pad[...] = jnp.zeros_like(hid_pad)
+    inner[...] = jnp.zeros_like(inner)
+    acc[...] = jnp.zeros_like(acc)
+    down_copy.wait()
+    hid_copy.wait()
+
+    def project(s):
+        for g in range(n_exp):
+            hid_pad[g * pad : g * pad + cap, :] = hid[s * n_exp + g].astype(F32)
+        saved = hid_pad[...].astype(BF)
+        for k in range(chunks):
+            y_ref[k, s] = dot(saved, down[:, k * width : (k + 1) * width])
+
+    def z_step(i, _):
+        k, d = i // steps, i % steps + 1
+
+        @pl.when(i < n_seq)
+        def _():
+            project(i)
+
+        z_take(k, d)
+
+        @pl.when(d < steps)
+        def _():
+            z_send(k, d)
+
+        @pl.when(d == steps)
+        def _():
+            block_in = gath[k].reshape(row_count, width)
+            rows[k, me] = dot(pick[...], block_in).astype(BF)
+            x_start(k, 0)
+
+            @pl.when(k >= 1)
+            def _():
+                x_take(k - 1, 0)
+                x_start(k - 1, 1)
+
+            pltpu.make_async_copy(
+                proj_hbm.at[:, pl.ds(0, width)], proj.at[k], proj_sem.at[k]
+            ).wait()
+            inner[...] += dot(gath[k].reshape(row_count, width), proj[k], ((1,), (1,)))
+
+        return 0
+
+    lax.fori_loop(0, chunks * steps, z_step, 0)
+    for s in range(chunks * steps, n_seq):
+        project(s)
+
+    left_of = lax.broadcasted_iota(jnp.int32, (1, lane), 1) < HEAD
+
+    def pair_step(j, _):
+        span = pl.ds(pl.multiple_of(j * lane, lane), lane)
+        cols = [column(cum_t[...], 2 * j + i) for i in range(2)]
+        rowv = [cum_ref[pl.ds(2 * j + i, 1), :] for i in range(2)]
+        steps_col = jnp.where(
+            left_of, column(step_t[...], 2 * j), column(step_t[...], 2 * j + 1)
+        )
+        col = jnp.where(left_of, cols[0], cols[1])
+        end_row = jnp.where(left_of, cols[0][row_count - 1 :], cols[1][row_count - 1 :])
+        fac[:, span] = steps_col * jnp.exp(end_row - col)
+        skip = skip_ref[:, span]
+        state = jnp.zeros((b_t.shape[1], lane), F32)
+        for i in reversed(range(blocks)):
+            lo, hi = i * block, (i + 1) * block
+            g = inner[lo:hi, span]
+            g_top, g_low = halves(g)
+            both = jnp.concatenate([g_top, g_low], axis=1)
+            parts, sums = [], []
+            for q in range(2):
+                r = rowv[q][:, lo:hi]
+                w = jnp.exp(jnp.minimum(r - cols[q][lo:hi], 0.0)) * bc[i]
+                w_top, w_low = halves(w)
+                x = dot(w_top, both)
+                parts.append(x[:, :lane] + x[:, lane:] + dot(w_low, g_top))
+                base = rowv[q][:, lo - 1 : lo] if i else jnp.zeros((1, 1), F32)
+                m_top, m_low = halves(c_ref[:, lo:hi] * jnp.exp(r - base))
+                x = dot(m_top, both)
+                sums.append(x[:, :lane] + x[:, lane:] + dot(m_low, g_top))
+            result = jnp.where(left_of, parts[0], parts[1])
+            if i < blocks - 1:
+                edge = col[hi - 1 : hi]
+                result += jnp.exp(edge - col[lo:hi]) * dot(b_t[lo:hi, :], state, precision=highest)
+            start = col[lo - 1 : lo] if i else jnp.zeros((1, lane), F32)
+            state = jnp.where(left_of, sums[0], sums[1]) + jnp.exp(col[hi - 1 : hi] - start) * state
+            inner[lo:hi, span] = steps_col[lo:hi] * result + skip * g
+        agg[0, : b_t.shape[1], span] = state
+        agg[0, b_t.shape[1] :, span] = jnp.broadcast_to(end_row, (8, lane))
+        return 0
+
+    def scores(k):
+        def one(s, _):
+            part = rows[k, s].astype(F32) * y_ref[k, s]
+            total = part[:, :128]
+            for i in range(1, width // 128):
+                total = total + part[:, i * 128 : (i + 1) * 128]
+            acc[s] += total
+            return 0
+
+        lax.fori_loop(0, n_seq, one, 0)
+
+    tasks = []
+    for stage in range(1, n_stage + 1):
+        for k in range(chunks):
+            if stage > 1 or k == chunks - 1:
+                tasks.append((k, stage))
+    tasks.sort(key=lambda t: (t[0] + 1.5 * t[1], t[0]))
+
+    def serve(count):
+        for _ in range(min(count, len(tasks))):
+            k, stage = tasks.pop(0)
+            x_take(k, stage - 1)
+            x_start(k, stage)
+
+    serve(1)
+    cut = pairs // 2
+    lax.fori_loop(0, cut, pair_step, 0)
+    serve(1)
+    lax.fori_loop(cut, pairs, pair_step, 0)
+
+    n_state = b_t.shape[1]
+    carry[...] = jnp.zeros_like(carry)
+    reach = jnp.zeros((1, channels), F32)
+
+    def a_copy(i, bit):
+        return pltpu.make_async_remote_copy(
+            src_ref=agg.at[i],
+            dst_ref=got.at[i],
+            send_sem=as_sem.at[i],
+            recv_sem=ar_sem.at[i],
+            device_id={"seq": flip(me, bit)},
+        )
+
+    order = [1] + bits
+    a_copy(0, 1).start()
+    for i, bit in enumerate(order):
+        serve(1)
+        a_copy(i, bit).wait_recv()
+        low = ((me // bit) % 2) == 0
+        other, other_t = got[i, :n_state, :], got[i, n_state : n_state + 1, :]
+        own, own_t = agg[i, :n_state, :], agg[i, n_state : n_state + 1, :]
+        carry[...] += jnp.where(low, jnp.exp(reach) * other, 0.0)
+        reach = reach + jnp.where(low, other_t, 0.0)
+        if i + 1 < len(order):
+            first = jnp.where(low, own, other)
+            first_t = jnp.where(low, own_t, other_t)
+            second = jnp.where(low, other, own)
+            agg[i + 1, :n_state, :] = first + jnp.exp(first_t) * second
+            agg[i + 1, n_state:, :] = jnp.broadcast_to(own_t + other_t, (8, channels))
+            a_copy(i + 1, order[i + 1]).start()
+
+    for i in range(blocks):
+        lo, hi = i * block, (i + 1) * block
+        from_carry = dot(b_t[lo:hi, :], carry[...], precision=highest)
+        out_ref[lo:hi, :] = (inner[lo:hi, :] + fac[lo:hi, :] * from_carry).astype(BF)
+
+    ready = [k for k in range(chunks) if (k, n_stage) not in tasks]
+    for k in range(chunks):
+        if k not in ready:
+            while (k, n_stage) in tasks:
+                serve(1)
+        x_take(k, n_stage)
+        scores(k)
+
+    def finish(s, _):
+        wide = jnp.transpose(acc[s])
+        score_ref[s] = jnp.sum(wide, axis=0, keepdims=True)
+        return 0
+
+    lax.fori_loop(0, n_seq, finish, 0)
+
+    for k in range(chunks):
+        for d in range(steps):
+            z_sent(k, d)
+        for stage in range(n_stage + 1):
+            for mine in x_copies(k, stage, True):
+                mine.wait_send()
+    for i, bit in enumerate(order):
+        a_copy(i, bit).wait_send()
+
+
+def plan(n_seq, n_exp, tok, depth, channels, cap, hidden, state):
+    pad = -(-cap // 8) * 8
+    chunks = 4
+    width = depth // chunks
+    shard = n_exp * pad
+    row_count = n_exp * tok
+    block = min(256, row_count)
+    heads = channels // HEAD
+    stages = n_seq.bit_length() - 1
+    steps = n_exp - 1
+    shapes = [
+        ((chunks, n_exp, tok, width), BF),
+        ((chunks, channels, width), BF),
+        ((n_seq * n_exp, cap, hidden), BF),
+        ((hidden, depth), BF),
+        ((chunks, n_seq, shard, width), F32),
+        ((chunks, n_seq, shard, width), BF),
+        ((shard, hidden), F32),
+        ((shard, row_count), BF),
+        ((row_count, channels), F32),
+        ((row_count, channels), F32),
+        ((n_seq, shard, 128), F32),
+        ((heads, row_count), F32),
+        ((row_count, heads), F32),
+        ((row_count, heads), F32),
+        ((row_count, state), F32),
+        ((row_count // block, block, block), F32),
+        ((stages, state + 8, channels), F32),
+        ((stages, state + 8, channels), F32),
+        ((state, channels), F32),
+    ]
+    total = 0
+    for shape, kind in shapes:
+        size = 1
+        for extent in shape:
+            size *= extent
+        total += size * (2 if kind is BF else 4)
+    fits = (
+        total < VMEM_ROOM - (8 << 20)
+        and n_seq & (n_seq - 1) == 0
+        and n_seq >= 4
+        and n_exp >= 2
+        and depth % (128 * chunks) == 0
+        and channels % (2 * HEAD) == 0
+        and row_count % block == 0
+        and tok % 8 == 0
+    )
+    sems = [
+        (chunks,), (), (), (chunks,),
+        (2, chunks, steps), (2, chunks, steps),
+        (chunks, n_seq - 1), (chunks, n_seq - 1),
+        (stages,), (stages,),
+    ]
+    return fits, (n_seq, n_exp, tok, cap, pad, chunks, width), shapes, sems
+
+
+def quick(
+    fitted, grad_out, out_proj, step_size, log_decay, b_input, c_output, skip_gain, expert_ids,
+    hidden_act, w_down,
+):
+    _, sizes, shapes, sems = fitted
+    n_seq, n_exp, tok, cap, pad, chunks, width = sizes
+    shard = n_exp * pad
+    vmem = pl.BlockSpec(memory_space=pltpu.VMEM)
+    hbm = pl.BlockSpec(memory_space=pl.ANY)
+    row_count, channels = n_exp * tok, out_proj.shape[0]
+    d_inner, table = pl.pallas_call(
+        functools.partial(fused, sizes),
+        out_shape=(
+            jax.ShapeDtypeStruct((row_count, channels), BF),
+            jax.ShapeDtypeStruct((n_seq, 1, shard), F32),
+        ),
+        in_specs=[hbm] * 4 + [vmem] * 6,
+        out_specs=(vmem, vmem),
+        scratch_shapes=[pltpu.VMEM(shape, kind) for shape, kind in shapes]
+        + [pltpu.SemaphoreType.DMA(s) if s else pltpu.SemaphoreType.DMA for s in sems],
+        compiler_params=pltpu.CompilerParams(
+            collective_id=0, has_side_effects=True, vmem_limit_bytes=VMEM_ROOM
+        ),
+    )(
+        grad_out, out_proj, hidden_act, w_down, step_size, log_decay, b_input, c_output,
+        skip_gain.reshape(1, -1), expert_ids,
+    )
+    exchanged = lax.all_to_all(
+        table.reshape(n_seq * n_exp, pad), ("seq", "exp"), split_axis=0, concat_axis=0, tiled=True
+    )
+    slot_table = jnp.sum(exchanged.reshape(n_seq, n_exp, pad), axis=0)
+    own_ids = lax.dynamic_slice_in_dim(expert_ids, lax.axis_index("exp") * tok, tok, 0)
+    d_gate = slot_lookup(slot_table, own_ids, pad, n_exp).T
+    return d_inner, d_gate
+
+
+def route(*args):
+    grad_out, out_proj, step_size, log_decay, b_input, c_output, skip_gain, ids, hidden, down = args
+    fitted = plan(
+        lax.axis_size("seq"), lax.axis_size("exp"), grad_out.shape[0], grad_out.shape[1],
+        out_proj.shape[0], hidden.shape[2], hidden.shape[3], b_input.shape[0],
+    )
+    if fitted[0]:
+        return quick(fitted, *args)
+    return shards(*args)
+
+
 def solution(mesh):
     in_specs = (
         P(("seq", "exp"), None),
@@ -171,4 +639,4 @@
         P("exp", "seq", None),
     )
     out_specs = (P("seq", "exp"), P(None, ("seq", "exp")))
-    return jax.shard_map(shards, mesh=mesh, in_specs=in_specs, out_specs=out_specs, check_vma=False)
+    return jax.shard_map(route, mesh=mesh, in_specs=in_specs, out_specs=out_specs, check_vma=False)

time: 208 us -> 111 us (0.53)
  Pallas kernels: 0 us -> 87.4 us
  matrix products: 50 us -> 0 us
  waiting for transfers between devices: 51.4 us -> 6.69 us
  blocking collectives: 40.1 us -> 0 us
  local copies, waits for them, and re-layouts: 34.5 us -> 10.8 us
  between operations: 14.9 us -> 0.7 us
  other arithmetic: 12 us -> 1.68 us
    pallas_call x0 -> x1, Pallas kernels: none -> 87.4 us  [quick(): pl.pallas_call(functools.partial(fused, sizes), out_shape=(jax.ShapeDtype...]
    dot_general x7 -> x0, matrix products: 50 us -> none  [the longest x1 20.5 us: block_pass(): jnp.einsum('hut,thp->uhp', weights * intersection[None], grad_block, prec...]
    all_gather x2 -> x0, waiting for transfers between devices: 48.2 us -> none  [the longest x1 46 us: shards(): gathered = lax.all_gather(grad_out, 'exp', axis=0, tiled=True)]
    unnamed x1 -> x0, blocking collectives: 23.5 us -> none
    convert_element_type x2 -> x0, local copies, waits for them, and re-layouts: 18.1 us -> none  [shards(): partial_scores = jnp.sum(projected * saved_rows.astype(jnp.float32), axis=1)]
    all_gather x1 -> x0, blocking collectives: 16.7 us -> none  [shards(): lax.all_gather(summary[None], 'seq', axis=0, tiled=True)]
    unnamed x24 -> x5, local copies, waits for them, and re-layouts: 2.13 us -> 9.91 us
    gather x1 -> x0, local copies, waits for them, and re-layouts: 6.22 us -> none  [shards(): slot_rows = jnp.take(gathered, flat_index, axis=0)]
  transfers between devices with their start and end apart: 3 -> 1, of which waited for: 3 -> 1; matrix products, arithmetic and copies ran while one was open for 22% -> 0% of each run, Pallas kernels for 0% -> 0%
where the time goes in v1:
time: 111 us
  Pallas kernels  87.4 us (79%)
  local copies, waits for them, and re-layouts  10.8 us (10%)
  waiting for transfers between devices  6.69 us (6%)
  starting transfers between devices  3.45 us (3%)
  other arithmetic  1.68 us (2%)
    pallas_call x1, Pallas kernels, quick(): pl.pallas_call(functools.partial(fused, sizes), out_shape=(jax.ShapeDtype...  87.4 us
    unnamed x5, local copies, waits for them, and re-layouts  9.91 us
    all_to_all x1, waiting for transfers between devices, quick(): lax.all_to_all(table.reshape(n_seq * n_exp, pad), ('seq', 'exp'), split_a...  6.69 us
    all_to_all x1, starting transfers between devices, quick(): lax.all_to_all(table.reshape(n_seq * n_exp, pad), ('seq', 'exp'), split_a...  3.45 us
  transfers between devices with their start and end apart: 1, of which 1 were waited for; matrix products, arithmetic and copies ran while one was open for 0% of the time, Pallas kernels for 0%

profile of v1, /device:TPU:0, one launch (start us, length us, event | category | flops | bytes accessed | tf_op | source)
XLA Modules:
  0.0 110.6 jit_solution(124925278847995061)
XLA Ops:
  0.6 0.0 copy-start
  0.6 6.8 %copy.19.hid_hbm = bf16[1,32,66,1024]{3,2,1,0:T(8,128)(2,1)} copy(bf16[1,32,66,1024]{3,1,2,0:T(8,128)(2,1)} %param.18) | data formatting | bytes 8650752 | tf_op args[8]
  7.4 0.0 copy-done
  7.4 0.9 copy.20.ids_ref
  8.3 87.4 %shard_map.113 = (bf16[512,1024]{1,0:T(8,128)(2,1)}, f32[8,1,288]{2,1,0:T(1,128)}) custom-call(bf16[128,2048]{1,0:T(8,128)(2,1)} %grad_hbm.1, bf16[1024,2048]{1,0:T(8,128)(2,1)} %proj_hbm.1, bf16[1,32,66,1024]{3,2,1,0:T(8,128)(2,1)} %copy.19.hid_hbm, bf16[1,1024,2048]{2,1,0:T(8,128)(2,1)} %down_hbm.1, f32[16,512]{1,0:T(8,128)} %step_ref.1, ...), custom_call_target="tpu_custom_call" | custom-call | tf_op jit(solution)/shard_map/pallas_call | solution.py:591
  95.7 0.7 reduce
  96.4 0.7 all_to_all.6
  97.1 3.4 %all-to-all-start = ((f32[32,1,72]{2,1,0:T(1,128)}), f32[32,1,72]{2,1,0:T(1,128)S(1)}, u32[]{:S(2)}, u32[]{:S(2)}) async-start(f32[32,1,72]{2,1,0:T(1,128)} %bitcast.1), calls=%async_computation | async-start | bytes 32768 | tf_op jit(solution)/shard_map/all_to_all | solution.py:608
  100.6 0.1 copy.21
  100.7 0.2 reduce_window_sum.11
  100.9 0.1 copy.22
  101.0 6.7 %all-to-all-done = f32[32,1,72]{2,1,0:T(1,128)S(1)} async-done(((f32[32,1,72]{2,1,0:T(1,128)}), f32[32,1,72]{2,1,0:T(1,128)S(1)}, u32[]{:S(2)}, u32[]{:S(2)}) %all-to-all-start) | async-done | bytes 9248 | tf_op jit(solution)/shard_map/all_to_all | solution.py:608
  107.7 0.1 select_reduce_fusion
  107.8 0.6 select_reduce_fusion.1
  108.4 2.3 %copy.25 = bf16[512,1024]{1,0:T(8,128)(2,1)} copy(bf16[512,1024]{1,0:T(8,128)(2,1)} %get-tuple-element.10) | data formatting | bytes 2097152
  (6 shorter events, 0.1 us)
Async XLA Ops:
  0.6 6.8 %copy-start = (s32[512,2]{0,1:T(2,128)S(1)}, s32[512,2]{0,1:T(2,128)}, u32[]{:S(2)}) copy-start(s32[512,2]{0,1:T(2,128)} %param.17) | copy-start | bytes 12292
  97.1 10.6 %all-to-all-start = ((f32[32,1,72]{2,1,0:T(1,128)}), f32[32,1,72]{2,1,0:T(1,128)S(1)}, u32[]{:S(2)}, u32[]{:S(2)}) async-start(f32[32,1,72]{2,1,0:T(1,128)} %bitcast.1), calls=%async_computation | async-start | bytes 32768 | tf_op jit(solution)/shard_map/all_to_all | solution.py:608

commit v2 on v1

--- a/solution.py
+++ b/solution.py
@@ -187,17 +187,19 @@
 def fused(
     sizes,
     grad_hbm, proj_hbm, hid_hbm, down_hbm, step_ref, decay_ref, b_ref, c_ref, skip_ref, ids_ref,
-    out_ref, score_ref,
-    gath, proj, hid, down, y_ref, rows, hid_pad, pick, inner, fac, acc,
-    cum_ref, cum_t, step_t, b_t, bc, agg, got, carry,
+    out_ref, table_ref,
+    gath, proj, hid, down, y_ref, rows, pick, inner, fac, acc,
+    cum_ref, cum_t, step_t, b_t, bc, agg, got, carry, mail, inbox,
     load_sem, hid_sem, down_sem, proj_sem,
-    zs_sem, zr_sem, xs_sem, xr_sem, as_sem, ar_sem,
+    zs_sem, zr_sem, xs_sem, xr_sem, as_sem, ar_sem, ms_sem, mr_sem,
 ):
-    n_seq, n_exp, tok, cap, pad, chunks, width = sizes
+    n_seq, n_exp, tok, cap, shard, chunks, width = sizes
     me = lax.axis_index("seq")
     z = lax.axis_index("exp")
-    shard = n_exp * pad
     row_count = n_exp * tok
+    spread = 2 * n_exp
+    n_dev = n_seq * n_exp
+    mine_id = me * n_exp + z
     bits = [1 << i for i in range(1, n_seq.bit_length() - 1)]
     n_stage = len(bits)
     steps = n_exp - 1
@@ -221,19 +223,16 @@
         ).start()
 
     barrier = pltpu.get_barrier_semaphore()
-    for bit in [1] + bits:
-        pl.semaphore_signal(barrier, inc=1, device_id={"seq": flip(me, bit)})
-
-    @pl.when(z > 0)
-    def _():
-        pl.semaphore_signal(barrier, inc=1, device_id={"exp": z - 1})
-
-    @pl.when(z < n_exp - 1)
-    def _():
-        pl.semaphore_signal(barrier, inc=1, device_id={"exp": z + 1})
-
-    ends = jnp.minimum(z, 1) + jnp.minimum(n_exp - 1 - z, 1)
-    pl.semaphore_wait(barrier, n_stage + 1 + ends)
+
+    def greet(i, _):
+        other = lax.rem(mine_id + i, n_dev)
+        pl.semaphore_signal(
+            barrier, inc=1, device_id={"seq": other // n_exp, "exp": lax.rem(other, n_exp)}
+        )
+        return 0
+
+    lax.fori_loop(1, n_dev, greet, 0)
+    pl.semaphore_wait(barrier, n_dev - 1)
 
     def z_copy(side, k, d, owner, target):
         return pltpu.make_async_remote_copy(
@@ -312,21 +311,18 @@
         for theirs in x_copies(k, stage, False):
             theirs.wait_recv()
 
-    ids = ids_ref[...]
-    hit = jnp.where(jnp.logical_or(ids[:, 0:1] == z, ids[:, 1:2] == z), 1.0, 0.0)
-    for i in range(2, ids.shape[1]):
-        hit = jnp.maximum(hit, jnp.where(ids[:, i : i + 1] == z, 1.0, 0.0))
+    hit = jnp.zeros((1, row_count), F32)
+    for i in range(ids_ref.shape[0]):
+        hit = jnp.maximum(hit, jnp.where(ids_ref[i : i + 1, :] == z, 1.0, 0.0))
     row_id = lax.broadcasted_iota(jnp.int32, (row_count, row_count), 0)
     col_id = lax.broadcasted_iota(jnp.int32, (row_count, row_count), 1)
-    same = jnp.logical_and(row_id // tok == col_id // tok, col_id < row_id)
-    before = dot(jnp.where(same, 1.0, 0.0).astype(BF), jnp.broadcast_to(hit, (row_count, 128)).astype(BF))
-    group = lax.broadcasted_iota(jnp.int32, (row_count, 1), 0) // tok
-    place = before[:, 0:1].astype(jnp.int32) + group * pad
-    slots = -(-shard // 128) * 128
-    chosen = jnp.logical_and(
-        lax.broadcasted_iota(jnp.int32, (row_count, slots), 1) == place, hit > 0.5
-    )
-    pick[...] = jnp.transpose(jnp.where(chosen, 1.0, 0.0))[:shard].astype(BF)
+    same = jnp.logical_and(row_id // tok == col_id // tok, row_id < col_id)
+    before = dot(jnp.broadcast_to(hit, (16, row_count)).astype(BF), jnp.where(same, 1.0, 0.0).astype(BF))
+    group = lax.broadcasted_iota(jnp.int32, (1, row_count), 1) // tok
+    place = before[0:1].astype(jnp.int32) * n_exp + group
+    place = jnp.where(hit > 0.5, place, -1)
+    chosen = lax.broadcasted_iota(jnp.int32, (shard, row_count), 0) == place
+    pick[...] = jnp.where(chosen, 1.0, 0.0).astype(BF)
 
     tri = jnp.where(row_id <= col_id, 1.0, 0.0)
     cum = dot(decay_ref[...], tri, precision=highest)
@@ -342,25 +338,38 @@
         cross = dot(b_t[span, :], c_ref[:, span], precision=highest)
         bc[i] = jnp.where(keep, cross, 0.0)
 
-    hid_pad[...] = jnp.zeros_like(hid_pad)
     inner[...] = jnp.zeros_like(inner)
     acc[...] = jnp.zeros_like(acc)
     down_copy.wait()
     hid_copy.wait()
 
-    def project(s):
-        for g in range(n_exp):
-            hid_pad[g * pad : g * pad + cap, :] = hid[s * n_exp + g].astype(F32)
-        saved = hid_pad[...].astype(BF)
+    group_count = hid.shape[1]
+    span_c = max(c for c in range(1, cap + 1) if cap % c == 0 and c * group_count <= 384)
+    parts_c = cap // span_c
+
+    def project(i):
+        span = pl.ds(i * span_c, span_c)
+        saved = hid[span].reshape(span_c * group_count, hid.shape[2])
         for k in range(chunks):
-            y_ref[k, s] = dot(saved, down[:, k * width : (k + 1) * width])
+            part = dot(saved, down[:, k * width : (k + 1) * width])
+            y_ref[k, span] = part.reshape(span_c, group_count, width)
 
     def z_step(i, _):
         k, d = i // steps, i % steps + 1
 
-        @pl.when(i < n_seq)
-        def _():
-            project(i)
+        @pl.when(jnp.logical_and(d == 1, k < parts_c))
+        def _():
+            project(k)
+
+        @pl.when(jnp.logical_and(d == 1, k >= 2))
+        def _():
+            x_take(k - 2, 1)
+            x_start(k - 2, 2)
+
+        @pl.when(jnp.logical_and(d == 2, k >= 1))
+        def _():
+            x_take(k - 1, 0)
+            x_start(k - 1, 1)
 
         z_take(k, d)
 
@@ -373,22 +382,16 @@
             block_in = gath[k].reshape(row_count, width)
             rows[k, me] = dot(pick[...], block_in).astype(BF)
             x_start(k, 0)
-
-            @pl.when(k >= 1)
-            def _():
-                x_take(k - 1, 0)
-                x_start(k - 1, 1)
-
             pltpu.make_async_copy(
                 proj_hbm.at[:, pl.ds(0, width)], proj.at[k], proj_sem.at[k]
             ).wait()
-            inner[...] += dot(gath[k].reshape(row_count, width), proj[k], ((1,), (1,)))
+            inner[...] += dot(block_in, proj[k], ((1,), (1,)))
 
         return 0
 
     lax.fori_loop(0, chunks * steps, z_step, 0)
-    for s in range(chunks * steps, n_seq):
-        project(s)
+    for i in range(chunks, parts_c):
+        project(i)
 
     left_of = lax.broadcasted_iota(jnp.int32, (1, lane), 1) < HEAD
 
@@ -431,21 +434,29 @@
         agg[0, b_t.shape[1] :, span] = jnp.broadcast_to(end_row, (8, lane))
         return 0
 
+    low_half = lax.broadcasted_iota(jnp.int32, (1, spread, width), 1) < n_exp
+
     def scores(k):
-        def one(s, _):
-            part = rows[k, s].astype(F32) * y_ref[k, s]
-            total = part[:, :128]
-            for i in range(1, width // 128):
-                total = total + part[:, i * 128 : (i + 1) * 128]
-            acc[s] += total
+        def one(p, _):
+            first = rows[k, 2 * p][: cap * n_exp].astype(F32).reshape(cap // 2, spread, width)
+            second = rows[k, 2 * p + 1][: cap * n_exp].astype(F32).reshape(cap // 2, spread, width)
+            even = jnp.where(low_half, first, pltpu.roll(second, n_exp, 1))
+            odd = jnp.where(low_half, pltpu.roll(first, n_exp, 1), second)
+            y = y_ref[k, :, pl.ds(pl.multiple_of(p * spread, spread), spread), :]
+            y = y.reshape(cap // 2, 2, spread, width)
+            for i, part in enumerate((even * y[:, 0], odd * y[:, 1])):
+                total = part[:, :, :128]
+                for j in range(1, width // 128):
+                    total = total + part[:, :, j * 128 : (j + 1) * 128]
+                acc[p, :, i] += total
             return 0
 
-        lax.fori_loop(0, n_seq, one, 0)
+        lax.fori_loop(0, n_seq // 2, one, 0)
 
     tasks = []
     for stage in range(1, n_stage + 1):
         for k in range(chunks):
-            if stage > 1 or k == chunks - 1:
+            if k + stage >= chunks:
                 tasks.append((k, stage))
     tasks.sort(key=lambda t: (t[0] + 1.5 * t[1], t[0]))
 
@@ -455,7 +466,6 @@
             x_take(k, stage - 1)
             x_start(k, stage)
 
-    serve(1)
     cut = pairs // 2
     lax.fori_loop(0, cut, pair_step, 0)
     serve(1)
@@ -477,7 +487,10 @@
     order = [1] + bits
     a_copy(0, 1).start()
     for i, bit in enumerate(order):
-        serve(1)
+        if i == 0:
+            serve(1)
+        x_take(i, n_stage)
+        scores(i)
         a_copy(i, bit).wait_recv()
         low = ((me // bit) % 2) == 0
         other, other_t = got[i, :n_state, :], got[i, n_state : n_state + 1, :]
@@ -497,20 +510,52 @@
         from_carry = dot(b_t[lo:hi, :], carry[...], precision=highest)
         out_ref[lo:hi, :] = (inner[lo:hi, :] + fac[lo:hi, :] * from_carry).astype(BF)
 
-    ready = [k for k in range(chunks) if (k, n_stage) not in tasks]
-    for k in range(chunks):
-        if k not in ready:
-            while (k, n_stage) in tasks:
-                serve(1)
+    for k in range(len(order), chunks):
+        if k == chunks - 2:
+            serve(len(tasks))
         x_take(k, n_stage)
         scores(k)
 
-    def finish(s, _):
-        wide = jnp.transpose(acc[s])
-        score_ref[s] = jnp.sum(wide, axis=0, keepdims=True)
+    def finish(p, _):
+        wide = jnp.transpose(acc[p].reshape(cap * spread, 128))
+        mail[p] = jnp.sum(wide, axis=0, keepdims=True)
         return 0
 
-    lax.fori_loop(0, n_seq, finish, 0)
+    lax.fori_loop(0, n_seq // 2, finish, 0)
+
+    def mail_copy(other, source, slot):
+        return pltpu.make_async_remote_copy(
+            src_ref=mail.at[other // spread],
+            dst_ref=inbox.at[source],
+            send_sem=ms_sem.at[slot],
+            recv_sem=mr_sem.at[source],
+            device_id={"seq": other // n_exp, "exp": lax.rem(other, n_exp)},
+        )
+
+    def post(i, _):
+        other = lax.rem(mine_id + i, n_dev)
+        mail_copy(other, mine_id, other).start()
+        return 0
+
+    def take(i, _):
+        other = lax.rem(mine_id + i, n_dev)
+        mail_copy(other, other, other).wait_recv()
+        return 0
+
+    def posted(i, _):
+        other = lax.rem(mine_id + i, n_dev)
+        mail_copy(other, mine_id, other).wait_send()
+        return 0
+
+    lax.fori_loop(1, n_dev, post, 0)
+    inbox[mine_id] = mail[me // 2]
+    lax.fori_loop(1, n_dev, take, 0)
+    for e in range(n_exp):
+        total = inbox[e]
+        for i in range(1, n_seq):
+            total = total + inbox[i * n_exp + e]
+        table_ref[e] = total
+    lax.fori_loop(1, n_dev, posted, 0)
 
     for k in range(chunks):
         for d in range(steps):
@@ -523,11 +568,11 @@
 
 
 def plan(n_seq, n_exp, tok, depth, channels, cap, hidden, state):
-    pad = -(-cap // 8) * 8
-    chunks = 4
+    chunks = 8
     width = depth // chunks
-    shard = n_exp * pad
+    shard = -(-cap * n_exp // 16) * 16
     row_count = n_exp * tok
+    letter = cap * n_exp * 2
     block = min(256, row_count)
     heads = channels // HEAD
     stages = n_seq.bit_length() - 1
@@ -535,15 +580,14 @@
     shapes = [
         ((chunks, n_exp, tok, width), BF),
         ((chunks, channels, width), BF),
-        ((n_seq * n_exp, cap, hidden), BF),
+        ((cap, n_seq * n_exp, hidden), BF),
         ((hidden, depth), BF),
-        ((chunks, n_seq, shard, width), F32),
+        ((chunks, cap, n_seq * n_exp, width), F32),
         ((chunks, n_seq, shard, width), BF),
-        ((shard, hidden), F32),
         ((shard, row_count), BF),
         ((row_count, channels), F32),
         ((row_count, channels), F32),
-        ((n_seq, shard, 128), F32),
+        ((n_seq // 2, cap // 2, 2, 2 * n_exp, 128), F32),
         ((heads, row_count), F32),
         ((row_count, heads), F32),
         ((row_count, heads), F32),
@@ -552,6 +596,8 @@
         ((stages, state + 8, channels), F32),
         ((stages, state + 8, channels), F32),
         ((state, channels), F32),
+        ((n_seq // 2, 1, letter), F32),
+        ((n_seq * n_exp, 1, letter), F32),
     ]
     total = 0
     for shape, kind in shapes:
@@ -562,8 +608,9 @@
     fits = (
         total < VMEM_ROOM - (8 << 20)
         and n_seq & (n_seq - 1) == 0
-        and n_seq >= 4
-        and n_exp >= 2
+        and stages == 3
+        and n_exp == 4
+        and cap % 2 == 0
         and depth % (128 * chunks) == 0
         and channels % (2 * HEAD) == 0
         and row_count % block == 0
@@ -574,8 +621,9 @@
         (2, chunks, steps), (2, chunks, steps),
         (chunks, n_seq - 1), (chunks, n_seq - 1),
         (stages,), (stages,),
+        (n_seq * n_exp,), (n_seq * n_exp,),
     ]
-    return fits, (n_seq, n_exp, tok, cap, pad, chunks, width), shapes, sems
+    return fits, (n_seq, n_exp, tok, cap, shard, chunks, width), shapes, sems
 
 
 def quick(
@@ -583,8 +631,7 @@
     hidden_act, w_down,
 ):
     _, sizes, shapes, sems = fitted
-    n_seq, n_exp, tok, cap, pad, chunks, width = sizes
-    shard = n_exp * pad
+    n_seq, n_exp, tok, cap, shard, chunks, width = sizes
     vmem = pl.BlockSpec(memory_space=pltpu.VMEM)
     hbm = pl.BlockSpec(memory_space=pl.ANY)
     row_count, channels = n_exp * tok, out_proj.shape[0]
@@ -592,7 +639,7 @@
         functools.partial(fused, sizes),
         out_shape=(
             jax.ShapeDtypeStruct((row_count, channels), BF),
-            jax.ShapeDtypeStruct((n_seq, 1, shard), F32),
+            jax.ShapeDtypeStruct((n_exp, 1, 2 * n_exp * cap), F32),
         ),
         in_specs=[hbm] * 4 + [vmem] * 6,
         out_specs=(vmem, vmem),
@@ -602,15 +649,21 @@
             collective_id=0, has_side_effects=True, vmem_limit_bytes=VMEM_ROOM
         ),
     )(
-        grad_out, out_proj, hidden_act, w_down, step_size, log_decay, b_input, c_output,
-        skip_gain.reshape(1, -1), expert_ids,
-    )
-    exchanged = lax.all_to_all(
-        table.reshape(n_seq * n_exp, pad), ("seq", "exp"), split_axis=0, concat_axis=0, tiled=True
-    )
-    slot_table = jnp.sum(exchanged.reshape(n_seq, n_exp, pad), axis=0)
-    own_ids = lax.dynamic_slice_in_dim(expert_ids, lax.axis_index("exp") * tok, tok, 0)
-    d_gate = slot_lookup(slot_table, own_ids, pad, n_exp).T
+        grad_out, out_proj, hidden_act.transpose(0, 2, 1, 3), w_down, step_size, log_decay, b_input, c_output,
+        skip_gain.reshape(1, -1), expert_ids.T,
+    )
+    exp_index = lax.axis_index("exp")
+    own_ids = lax.dynamic_slice_in_dim(expert_ids, exp_index * tok, tok, 0)
+    group = lax.rem(lax.axis_index("seq"), 2) * n_exp + exp_index
+    experts = lax.broadcasted_iota(jnp.int32, (1, 1, n_exp), 2)
+    onehot = own_ids[:, :, None] == experts
+    member = jnp.any(onehot, axis=1).astype(jnp.int32)
+    rank_ids = jnp.cumsum(member, axis=0) - 1
+    slot_of = jnp.sum(jnp.where(onehot, rank_ids[:, None, :], 0), axis=2)
+    spot = own_ids * table.shape[2] + slot_of * (2 * n_exp) + group
+    flat = table.reshape(1, 1, -1)
+    spots = lax.broadcasted_iota(jnp.int32, flat.shape, 2)
+    d_gate = jnp.sum(jnp.where(spots == spot.T[:, :, None], flat, 0.0), axis=2)
     return d_inner, d_gate
 
 

time: 111 us -> 121 us (1.090)
  Pallas kernels: 87.4 us -> 114 us
  local copies, waits for them, and re-layouts: 10.8 us -> 3.2 us
  waiting for transfers between devices: 6.69 us -> 0 us
  starting transfers between devices: 3.45 us -> 0 us
    pallas_call x1, Pallas kernels: 87.4 us -> 114 us  [quick(): pl.pallas_call(functools.partial(fused, sizes), out_shape=(jax.ShapeDtype...]
    unnamed x5 -> x1, local copies, waits for them, and re-layouts: 9.91 us -> 2.26 us
    all_to_all x1 -> x0, waiting for transfers between devices: 6.69 us -> none  [quick(): lax.all_to_all(table.reshape(n_seq * n_exp, pad), ('seq', 'exp'), split_a...]
    all_to_all x1 -> x0, starting transfers between devices: 3.45 us -> none  [quick(): lax.all_to_all(table.reshape(n_seq * n_exp, pad), ('seq', 'exp'), split_a...]
  transfers between devices with their start and end apart: 1 -> 0, of which waited for: 1 -> 0; matrix products, arithmetic and copies ran while one was open for 0% -> 0% of each run, Pallas kernels for 0% -> 0%
where the time goes in v2:
time: 121 us; the launch traced here: 120 us
  Pallas kernels  114 us (94%)
  local copies, waits for them, and re-layouts  3.2 us (3%)
  other arithmetic  2.59 us (2%)
    pallas_call x1, Pallas kernels, quick(): pl.pallas_call(functools.partial(fused, sizes), out_shape=(jax.ShapeDtype...  114 us

profile of v2, /device:TPU:0, one launch (start us, length us, event | category | flops | bytes accessed | tf_op | source)
XLA Modules:
  0.0 120.5 jit_solution(10554913144055477141)
XLA Ops:
  0.6 0.7 constant_dynamic-slice_fusion
  1.3 0.1 copy.13
  1.5 0.2 reduce_window_sum.11
  1.6 0.1 copy.14
  1.7 0.7 add_bitcast_fusion
  2.4 114.0 %shard_map.113 = (bf16[512,1024]{1,0:T(8,128)(2,1)}, f32[4,1,528]{2,1,0:T(1,128)}) custom-call(bf16[128,2048]{1,0:T(8,128)(2,1)} %grad_hbm.1, bf16[1024,2048]{1,0:T(8,128)(2,1)} %proj_hbm.1, bf16[1,66,32,1024]{3,2,1,0:T(8,128)(2,1)} %bitcast.5, bf16[1,1024,2048]{2,1,0:T(8,128)(2,1)} %down_hbm.1, f32[16,512]{1,0:T(8,128)} %step_ref.1, f32[16,512]{1,0:T(8,128)} %decay_ref.1, ...), custom_call_target="tpu_custom_call" | custom-call | tf_op jit(solution)/shard_map/pallas_call | solution.py:638
  116.4 0.7 reduce
  117.2 0.1 broadcast_in_dim.31
  117.3 0.9 select_reduce_fusion
  118.2 2.3 %copy.16 = bf16[512,1024]{1,0:T(8,128)(2,1)} copy(bf16[512,1024]{1,0:T(8,128)(2,1)} %get-tuple-element.8) | data formatting | bytes 2097152
  (4 shorter events, 0.1 us)

commit v3 on v2

--- a/solution.py
+++ b/solution.py
@@ -274,7 +274,8 @@
         pltpu.make_async_copy(
             grad_hbm.at[:, pl.ds(k * width, width)], gath.at[k, z], load_sem.at[k]
         ).wait()
-        z_send(k, 0)
+        if k == 0:
+            z_send(k, 0)
 
     def bit_of(k, stage):
         if stage == n_stage:
@@ -356,10 +357,15 @@
 
     def z_step(i, _):
         k, d = i // steps, i % steps + 1
-
-        @pl.when(jnp.logical_and(d == 1, k < parts_c))
-        def _():
-            project(k)
+        z_take(k, d)
+
+        @pl.when(d < steps)
+        def _():
+            z_send(k, d)
+
+        @pl.when(jnp.logical_and(d == 1, k < chunks - 1))
+        def _():
+            z_send(k + 1, 0)
 
         @pl.when(jnp.logical_and(d == 1, k >= 2))
         def _():
@@ -371,11 +377,9 @@
             x_take(k - 1, 0)
             x_start(k - 1, 1)
 
-        z_take(k, d)
-
-        @pl.when(d < steps)
-        def _():
-            z_send(k, d)
+        @pl.when(jnp.logical_and(d == 1, k < parts_c))
+        def _():
+            project(k)
 
         @pl.when(d == steps)
         def _():
@@ -489,6 +493,8 @@
     for i, bit in enumerate(order):
         if i == 0:
             serve(1)
+        while (i, n_stage) in tasks:
+            serve(1)
         x_take(i, n_stage)
         scores(i)
         a_copy(i, bit).wait_recv()
@@ -511,7 +517,7 @@
         out_ref[lo:hi, :] = (inner[lo:hi, :] + fac[lo:hi, :] * from_carry).astype(BF)
 
     for k in range(len(order), chunks):
-        if k == chunks - 2:
+        if k >= chunks - 2:
             serve(len(tasks))
         x_take(k, n_stage)
         scores(k)

time: 121 us -> 108 us (0.89)
  Pallas kernels: 114 us -> 101 us
    pallas_call x1, Pallas kernels: 114 us -> 101 us  [quick(): pl.pallas_call(functools.partial(fused, sizes), out_shape=(jax.ShapeDtype...]
where the time goes in v3:
time: 108 us
  Pallas kernels  101 us (94%)
  local copies, waits for them, and re-layouts  3.2 us (3%)
  other arithmetic  2.59 us (2%)
    pallas_call x1, Pallas kernels, quick(): pl.pallas_call(functools.partial(fused, sizes), out_shape=(jax.ShapeDtype...  101 us
    unnamed x1, local copies, waits for them, and re-layouts  2.26 us

profile of v3, /device:TPU:0, one launch (start us, length us, event | category | flops | bytes accessed | tf_op | source)
XLA Modules:
  0.0 107.5 jit_solution(10073882231246933455)
XLA Ops:
  0.6 0.7 constant_dynamic-slice_fusion
  1.3 0.1 copy.13
  1.5 0.2 reduce_window_sum.11
  1.6 0.1 copy.14
  1.7 0.7 add_bitcast_fusion
  2.4 101.1 %shard_map.113 = (bf16[512,1024]{1,0:T(8,128)(2,1)}, f32[4,1,528]{2,1,0:T(1,128)}) custom-call(bf16[128,2048]{1,0:T(8,128)(2,1)} %grad_hbm.1, bf16[1024,2048]{1,0:T(8,128)(2,1)} %proj_hbm.1, bf16[1,66,32,1024]{3,2,1,0:T(8,128)(2,1)} %bitcast.5, bf16[1,1024,2048]{2,1,0:T(8,128)(2,1)} %down_hbm.1, f32[16,512]{1,0:T(8,128)} %step_ref.1, f32[16,512]{1,0:T(8,128)} %decay_ref.1, ...), custom_call_target="tpu_custom_call" | custom-call | tf_op jit(solution)/shard_map/pallas_call | solution.py:644
  103.5 0.7 reduce
  104.2 0.1 broadcast_in_dim.31
  104.3 0.9 select_reduce_fusion
  105.3 2.3 %copy.16 = bf16[512,1024]{1,0:T(8,128)(2,1)} copy(bf16[512,1024]{1,0:T(8,128)(2,1)} %get-tuple-element.8) | data formatting | bytes 2097152
  (4 shorter events, 0.1 us)
